TPU v7x, 32 devices: a whole 2x2x4 slice. The times are simulated.
32 devices in a mesh: types: 16 (over z, y, x), tm: 2 (over core).
Axes of the slice: x: 2, y: 2, z: 4, core: 2. Of those that a mesh axis runs over, the one named last changes fastest.
Arguments:
- brackets: int32 [96, 8, 7, 512], P('types', 'tm'), may hold values from 0 to 510, as said below
- active_blocks: int32 [96], P('types'), may hold values from 1 to 4, as said below
- initial_mass: float32 [96, 7, 512], P('types'), may hold values from 0 to 0.00055803574
- patience: float32 [96], P('types'), may hold values from 0.9 to 0.985
- productivity: float32 [96], P('types'), may hold values from 0.5 to 2
- income_levels: float32 [7], replicated, may hold values from 0.3 to 3
- income_transition: float32 [7, 7], replicated, may hold values from 0 to 1, as said below
- wage_path: float32 [8], replicated, may hold values from 0.8 to 1.2
- bond_supply: float32 [8], replicated, may hold values from 0.5 to 2
- price_guess: float32 [8], replicated, may hold values from -3 to 3
- jac_inverse: float32 [8, 8], replicated, may hold values from -2 to 2
- assignment: int32 [96], replicated, may hold values from 0 to 95, each once
Outputs:
- price_path: float32 [8], replicated
- market_gap: float32 [8], replicated
- type_paths: float32 [96, 2, 8], P('types')
Inputs may be any that keep to these rules, and one draw needn't show every extreme that they name: `brackets`: the bracket of asset point i lies between max(i - 9, 0) and max(i - 1, 0). `active_blocks`: counts of 128-point blocks from the bottom of the grid. `income_transition`: rows of positive entries summing to one. `assignment`: each type appears once.
All inputs are finite; a program needn't handle non-finite values.
Results may differ from a plain program's by a relative error of at most 0.0003.
Values sent between devices are 32-bit elements; how exact they have to be, the bound alone decides.
A program may use at most 64 MiB of HBM per device.

v0:
```python
import jax
import jax.numpy as jnp
from jax import lax
from jax.sharding import PartitionSpec as P

ASSETS = 512
BLOCK = 128
NEWTON = 2
grid_top = 40.0
rate_floor = 0.005
rate_span = 0.03
highest = lax.Precision.HIGHEST


def asset_grid(points):
    return grid_top * (points / (ASSETS - 1)) ** 2


def interest(price_path):
    return rate_floor + rate_span * jax.nn.sigmoid(price_path)


def policy(lower_edge, upper_edge, bracket_now, rate_now, income_now, grid_rows):
    grid_low = asset_grid(bracket_now.astype(jnp.float32))
    grid_high = asset_grid((bracket_now + 1).astype(jnp.float32))
    spacing = jnp.maximum(upper_edge - lower_edge, (grid_high - grid_low) / (1.0 + rate_now))
    weight_up = jnp.clip((grid_rows[None, :] - lower_edge) / spacing, 0.0, 1.0)
    savings = grid_low + weight_up * (grid_high - grid_low)
    spending = (1.0 + rate_now) * grid_rows[None, :] + income_now[:, None] - savings
    return (weight_up, savings, spending)


def band_table(bracket_rows, window):
    targets = window + jnp.arange(2 * BLOCK, dtype=jnp.int32)
    return (bracket_rows[:, :, None] == targets[None, None, :]).astype(jnp.float32)


def backward_type(bracket, blocks, patience, incomes, interest_path, values_end, transition):
    grid_values = asset_grid(jnp.arange(ASSETS, dtype=jnp.float32))
    income_count = values_end.shape[0]

    def backward_period(values, inputs):
        bracket_now, rate_now, income_now = inputs
        expected = patience * jnp.dot(transition, values, precision=highest)
        endogenous = (1.0 / expected + grid_values[None, :] - income_now[:, None]) / (
            1.0 + rate_now
        )
        following = jnp.concatenate([endogenous[:, 1:], endogenous[:, -1:]], axis=1)
        stacked = jnp.stack([endogenous, following])

        def backward_block_rows(block_index, carried):
            row_start = block_index * BLOCK
            window = jnp.maximum(row_start - BLOCK, 0)
            bracket_rows = lax.dynamic_slice_in_dim(bracket_now, row_start, BLOCK, 1)
            onehot = band_table(bracket_rows, window)
            stacked_window = lax.dynamic_slice_in_dim(stacked, window, 2 * BLOCK, 2)
            picked = jnp.einsum("eia,cea->cei", onehot, stacked_window, precision=highest)
            grid_rows = lax.dynamic_slice_in_dim(grid_values, row_start, BLOCK, 0)
            weight_up, savings, spending = policy(
                picked[0], picked[1], bracket_rows, rate_now, income_now, grid_rows
            )
            fresh = (weight_up, savings, spending, (1.0 + rate_now) / spending)
            return tuple(
                (
                    lax.dynamic_update_slice_in_dim(target_array, piece_array, row_start, 1)
                    for target_array, piece_array in zip(carried, fresh)
                )
            )

        zeros_rows = jnp.zeros((income_count, ASSETS), jnp.float32)
        ones_rows = jnp.ones((income_count, ASSETS), jnp.float32)
        weight_up, savings, spending, values_new = lax.fori_loop(
            0, blocks, backward_block_rows, (zeros_rows, zeros_rows, ones_rows, ones_rows)
        )
        return (values_new, (weight_up, savings, spending))

    return lax.scan(backward_period, values_end, (bracket, interest_path, incomes), reverse=True)


def forward_type(bracket, blocks, weight_up, savings, spending, mass_start, transition):

    def forward_period(masses, inputs):
        bracket_now, weight_now, savings_now, spending_now = inputs
        totals = jnp.stack([jnp.sum(masses * savings_now), jnp.sum(masses * spending_now)])
        weights = jnp.stack([(1.0 - weight_now) * masses, weight_now * masses])

        def forward_block_rows(block_index, shifted_mass):
            row_start = block_index * BLOCK
            window = jnp.maximum(row_start - BLOCK, 0)
            bracket_rows = lax.dynamic_slice_in_dim(bracket_now, row_start, BLOCK, 1)
            onehot = band_table(bracket_rows, window)
            weight_rows = lax.dynamic_slice_in_dim(weights, row_start, BLOCK, 2)
            contrib = jnp.einsum("eia,cei->cea", onehot, weight_rows, precision=highest)
            current = lax.dynamic_slice_in_dim(shifted_mass, window, 2 * BLOCK, 2)
            return lax.dynamic_update_slice_in_dim(shifted_mass, current + contrib, window, 2)

        shifted_mass = lax.fori_loop(0, blocks, forward_block_rows, jnp.zeros_like(weights))
        arrived = shifted_mass[0] + jnp.concatenate(
            [jnp.zeros_like(shifted_mass[1][:, :1]), shifted_mass[1][:, :-1]], axis=1
        )
        return (jnp.dot(transition.T, arrived, precision=highest), totals)

    masses_end, type_series = lax.scan(
        forward_period, mass_start, (bracket, weight_up, savings, spending)
    )
    return (masses_end, type_series.T)


def body(
    brackets,
    active_blocks,
    initial_mass,
    patience,
    productivity,
    income_levels,
    income_transition,
    wage_path,
    bond_supply,
    price_guess,
    jac_inverse,
    assignment,
):
    local_types = patience.shape[0]
    all_types = local_types * lax.axis_size("types")
    core_count = lax.axis_size("tm")
    core_index = lax.axis_index("tm")
    columns = jnp.arange(ASSETS, dtype=jnp.int32)
    grid_values = asset_grid(columns.astype(jnp.float32))
    type_numbers = (
        lax.axis_index("types") * local_types + jnp.arange(local_types, dtype=jnp.int32)
    ).astype(jnp.float32)
    half_types = local_types // core_count
    brackets_mine = lax.all_to_all(brackets, "tm", split_axis=0, concat_axis=1, tiled=True)

    def take_mine(target_array):
        return lax.dynamic_slice_in_dim(target_array, core_index * half_types, half_types, 0)

    blocks_mine = take_mine(active_blocks)
    patience_mine = take_mine(patience)
    productivity_mine = take_mine(productivity)
    mass_mine = take_mine(initial_mass)
    numbers_mine = take_mine(type_numbers)
    live_rows = (columns[None, None, :] < blocks_mine[:, None, None] * BLOCK).astype(jnp.float32)
    mass_start = mass_mine * live_rows
    price_path = price_guess
    market_gap = jnp.zeros_like(price_guess)
    everything = None
    for newton_round in range(NEWTON):
        interest_path = interest(price_path)
        last_rate = interest_path[-1]
        ends_income = wage_path[-1] * productivity_mine[:, None] * income_levels[None, :]
        values_end = (1.0 + last_rate) / (
            last_rate * grid_values[None, None, :] + ends_income[:, :, None]
        )
        interest_here = interest_path
        incomes = (
            wage_path[None, :, None]
            * productivity_mine[:, None, None]
            * income_levels[None, None, :]
        )

        def sweep_solve_member(members):
            return backward_type(
                members[0],
                members[1],
                members[2],
                members[3],
                interest_here,
                members[4],
                income_transition,
            )

        values_start, solve_policies = lax.map(
            sweep_solve_member, (brackets_mine, blocks_mine, patience_mine, incomes, values_end)
        )

        def solve_member(members):
            return forward_type(
                members[0],
                members[1],
                members[2],
                members[3],
                members[4],
                members[5],
                income_transition,
            )

        masses_end, solve_type_series = lax.map(
            solve_member,
            (
                brackets_mine,
                blocks_mine,
                solve_policies[0],
                solve_policies[1],
                solve_policies[2],
                mass_start,
            ),
        )
        local_sum = jnp.sum(solve_type_series[:, 0, :], axis=0)
        totals = lax.psum(local_sum, ("types", "tm"))
        if newton_round + 1 == NEWTON:
            everything = (
                lax.all_gather(solve_type_series, ("types", "tm"), axis=0, tiled=True),
                lax.all_gather(numbers_mine, ("types", "tm"), axis=0, tiled=True),
            )
        market_gap = totals / all_types - bond_supply
        price_path = price_path - jnp.dot(jac_inverse, market_gap, precision=highest)
    slot_types = lax.dynamic_slice_in_dim(
        assignment, lax.axis_index("types") * local_types, local_types, 0
    ).astype(jnp.float32)
    select = (slot_types[:, None] == everything[1][None, :]).astype(jnp.float32)
    type_paths = jnp.einsum("st,tcp->scp", select, everything[0], precision=highest)
    return (price_path, market_gap, type_paths)


def solution(mesh):
    placed = (
        P("types", "tm", None, None),
        P("types"),
        P("types", None, None),
        P("types"),
        P("types"),
        P(),
        P(),
        P(),
        P(),
        P(),
        P(),
        P(),
    )
    return jax.shard_map(
        body,
        mesh=mesh,
        in_specs=placed,
        out_specs=(P(), P(), P("types", None, None)),
        check_vma=False,
    )
```

profile of v0, /device:TPU:14, one launch (start us, length us, event | category | flops | bytes accessed | tf_op | source)
XLA Modules:
  0.0 985.2 jit_solution(13439941722664523661)
XLA Ops:
  12.0 147.5 %while.321 = (s32[]{:T(128)}, f32[3,8,7,512]{3,2,1,0:T(8,128)S(1)}, f32[3,8,7,512]{3,2,1,0:T(8,128)S(1)}, f32[3,8,7,512]{3,2,1,0:T(8,128)S(1)}, f32[3,7,512]{2,1...) while((s32[]{:T(128)}, f32[3,8,7,512]{3,2,1,0:T(8,128)S(1)}, ...), condition=%wide.region_5.6_spmd, body=%wide.region_0.5_spmd.sunk | while | flops 6097422 | bytes 1872705 | solution.py:173
  13.4 47.7 %while.328 = (s32[]{:T(128)}, f32[7,512]{1,0:T(8,128)S(1)}, f32[8,7,512]{2,1,0:T(8,128)S(1)}, f32[8,7,512]{2,1,0:T(8,128)S(1)}, f32[8,7,512]{2,1,0:T(8,128)S(1)}...) while((s32[]{:T(128)}, f32[7,512]{1,0:T(8,128)S(1)}, ...), condition=%wide.region_4.4_spmd.clone.clone, body=%wide.region_1.3_spmd.clone.clone.sunk | while | flops 6097420 | bytes 483244 | solution.py:77
  21.7 3.6 while.335
  27.7 3.6 while.335
  62.6 47.7 %while.328 = (s32[]{:T(128)}, f32[7,512]{1,0:T(8,128)S(1)}, f32[8,7,512]{2,1,0:T(8,128)S(1)}, f32[8,7,512]{2,1,0:T(8,128)S(1)}, f32[8,7,512]{2,1,0:T(8,128)S(1)}...) while((s32[]{:T(128)}, f32[7,512]{1,0:T(8,128)S(1)}, ...), condition=%wide.region_4.4_spmd.clone.clone, body=%wide.region_1.3_spmd.clone.clone.sunk | while | flops 6097420 | bytes 483244 | solution.py:77
  70.9 3.6 while.335
  76.8 3.6 while.335
  106.7 3.6 while.335
  111.8 47.7 %while.328 = (s32[]{:T(128)}, f32[7,512]{1,0:T(8,128)S(1)}, f32[8,7,512]{2,1,0:T(8,128)S(1)}, f32[8,7,512]{2,1,0:T(8,128)S(1)}, f32[8,7,512]{2,1,0:T(8,128)S(1)}...) while((s32[]{:T(128)}, f32[7,512]{1,0:T(8,128)S(1)}, ...), condition=%wide.region_4.4_spmd.clone.clone, body=%wide.region_1.3_spmd.clone.clone.sunk | while | flops 6097420 | bytes 483244 | solution.py:77
  114.1 3.6 while.335
  120.1 3.6 while.335
  149.9 3.6 while.335
  155.9 3.6 while.335
  159.7 143.2 %while.323 = (s32[]{:T(128)}, f32[3,2,8]{2,1,0:T(2,128)S(1)}, f32[3,7,512]{2,1,0:T(8,128)S(1)}, s32[3,8,7,512]{3,2,1,0:T(8,128)S(1)}, f32[3,8,7,512]{3,2,1,0:T(8...) while((s32[]{:T(128)}, f32[3,2,8]{2,1,0:T(2,128)S(1)}, ...), condition=%wide.region_13.14_spmd, body=%wide.region_6.13_spmd.sunk | while | flops 6075148 | bytes 1450953 | solution.py:188
  160.4 46.9 %while.329 = (s32[]{:T(128)}, f32[7,512]{1,0:T(8,128)S(1)}, f32[8,2]{1,0:T(8,128)S(1)}, s32[8,7,512]{2,1,0:T(8,128)S(1)}, f32[8,7,512]{2,1,0:T(8,128)S(1)}, /*in...) while((s32[]{:T(128)}, f32[7,512]{1,0:T(8,128)S(1)}, ...), condition=%wide.region_12.12_spmd, body=%wide.region_7.11_spmd.sunk | while | flops 6075146 | bytes 502252 | solution.py:103
  208.1 46.9 %while.329 = (s32[]{:T(128)}, f32[7,512]{1,0:T(8,128)S(1)}, f32[8,2]{1,0:T(8,128)S(1)}, s32[8,7,512]{2,1,0:T(8,128)S(1)}, f32[8,7,512]{2,1,0:T(8,128)S(1)}, /*in...) while((s32[]{:T(128)}, f32[7,512]{1,0:T(8,128)S(1)}, ...), condition=%wide.region_12.12_spmd, body=%wide.region_7.11_spmd.sunk | while | flops 6075146 | bytes 502252 | solution.py:103
  255.8 46.9 %while.329 = (s32[]{:T(128)}, f32[7,512]{1,0:T(8,128)S(1)}, f32[8,2]{1,0:T(8,128)S(1)}, s32[8,7,512]{2,1,0:T(8,128)S(1)}, f32[8,7,512]{2,1,0:T(8,128)S(1)}, /*in...) while((s32[]{:T(128)}, f32[7,512]{1,0:T(8,128)S(1)}, ...), condition=%wide.region_12.12_spmd, body=%wide.region_7.11_spmd.sunk | while | flops 6075146 | bytes 502252 | solution.py:103
  302.9 174.0 %psum.14 = f32[8]{0:T(128)S(1)} all-reduce(f32[8]{0:T(128)S(1)} %slice_reduce_fusion.1), channel_id=1, replica_groups=mesh['types'=16,'tm'=2] {'types','tm'}, use_global_device_ids=true, to_apply=%region_15.16 | all-reduce | flops 8 | bytes 64 | tf_op jit(solution)/shard_map/psum | solution.py:200
  479.2 147.6 %while.325 = (s32[]{:T(128)}, f32[3,8,7,512]{3,2,1,0:T(8,128)S(1)}, f32[3,8,7,512]{3,2,1,0:T(8,128)S(1)}, f32[3,8,7,512]{3,2,1,0:T(8,128)S(1)}, f32[3,7,512]{2,1...) while((s32[]{:T(128)}, f32[3,8,7,512]{3,2,1,0:T(8,128)S(1)}, ...), condition=%wide.region_21.22_spmd, body=%wide.region_16.21_spmd.sunk | while | flops 6097422 | bytes 1872697 | solution.py:173
  480.6 47.7 %while.330 = (s32[]{:T(128)}, f32[7,512]{1,0:T(8,128)S(1)}, f32[8,7,512]{2,1,0:T(8,128)S(1)}, f32[8,7,512]{2,1,0:T(8,128)S(1)}, f32[8,7,512]{2,1,0:T(8,128)S(1)}...) while((s32[]{:T(128)}, f32[7,512]{1,0:T(8,128)S(1)}, ...), condition=%wide.region_20.20_spmd.clone.clone, body=%wide.region_17.19_spmd.clone.clone.sunk | while | flops 6097420 | bytes 483244 | solution.py:77
  482.9 3.6 while.333
  518.7 3.6 while.333
  524.6 3.6 while.333
  529.8 47.7 %while.330 = (s32[]{:T(128)}, f32[7,512]{1,0:T(8,128)S(1)}, f32[8,7,512]{2,1,0:T(8,128)S(1)}, f32[8,7,512]{2,1,0:T(8,128)S(1)}, f32[8,7,512]{2,1,0:T(8,128)S(1)}...) while((s32[]{:T(128)}, f32[7,512]{1,0:T(8,128)S(1)}, ...), condition=%wide.region_20.20_spmd.clone.clone, body=%wide.region_17.19_spmd.clone.clone.sunk | while | flops 6097420 | bytes 483244 | solution.py:77
  538.0 3.6 while.333
  578.9 47.7 %while.330 = (s32[]{:T(128)}, f32[7,512]{1,0:T(8,128)S(1)}, f32[8,7,512]{2,1,0:T(8,128)S(1)}, f32[8,7,512]{2,1,0:T(8,128)S(1)}, f32[8,7,512]{2,1,0:T(8,128)S(1)}...) while((s32[]{:T(128)}, f32[7,512]{1,0:T(8,128)S(1)}, ...), condition=%wide.region_20.20_spmd.clone.clone, body=%wide.region_17.19_spmd.clone.clone.sunk | while | flops 6097420 | bytes 483244 | solution.py:77
  626.8 143.2 %while.327 = (s32[]{:T(128)}, f32[3,2,8]{2,1,0:T(2,128)S(1)}, f32[3,7,512]{2,1,0:T(8,128)S(1)}, s32[3,8,7,512]{3,2,1,0:T(8,128)S(1)}, f32[3,8,7,512]{3,2,1,0:T(8...) while((s32[]{:T(128)}, f32[3,2,8]{2,1,0:T(2,128)S(1)}, ...), condition=%wide.region_29.30_spmd, body=%wide.region_22.29_spmd.sunk | while | flops 6075148 | bytes 1450953 | solution.py:188
  627.5 46.9 %while.331 = (s32[]{:T(128)}, f32[7,512]{1,0:T(8,128)S(1)}, f32[8,2]{1,0:T(8,128)S(1)}, s32[8,7,512]{2,1,0:T(8,128)S(1)}, f32[8,7,512]{2,1,0:T(8,128)S(1)}, /*in...) while((s32[]{:T(128)}, f32[7,512]{1,0:T(8,128)S(1)}, ...), condition=%wide.region_28.28_spmd, body=%wide.region_23.27_spmd.sunk | while | flops 6075146 | bytes 502252 | solution.py:103
  675.2 46.9 %while.331 = (s32[]{:T(128)}, f32[7,512]{1,0:T(8,128)S(1)}, f32[8,2]{1,0:T(8,128)S(1)}, s32[8,7,512]{2,1,0:T(8,128)S(1)}, f32[8,7,512]{2,1,0:T(8,128)S(1)}, /*in...) while((s32[]{:T(128)}, f32[7,512]{1,0:T(8,128)S(1)}, ...), condition=%wide.region_28.28_spmd, body=%wide.region_23.27_spmd.sunk | while | flops 6075146 | bytes 502252 | solution.py:103
  722.9 46.9 %while.331 = (s32[]{:T(128)}, f32[7,512]{1,0:T(8,128)S(1)}, f32[8,2]{1,0:T(8,128)S(1)}, s32[8,7,512]{2,1,0:T(8,128)S(1)}, f32[8,7,512]{2,1,0:T(8,128)S(1)}, /*in...) while((s32[]{:T(128)}, f32[7,512]{1,0:T(8,128)S(1)}, ...), condition=%wide.region_28.28_spmd, body=%wide.region_23.27_spmd.sunk | while | flops 6075146 | bytes 502252 | solution.py:103
  770.0 166.2 %all_gather.7 = f32[96,2,8]{2,1,0:T(2,128)S(1)} all-gather(f32[3,2,8]{2,1,0:T(2,128)S(1)} %get-tuple-element.1994), channel_id=1, replica_groups=mesh['types'=16,'tm'=2] {'types','tm'}, dimensions={0}, use_global_device_ids=true | all-gather | bytes 6336 | tf_op jit(solution)/shard_map/all_gather | solution.py:203
  936.2 46.3 %all-reduce.3 = (f32[8]{0:T(128)S(1)}, f32[96]{0:T(128)S(1)}) all-reduce(f32[8]{0:T(128)S(1)} %slice_reduce_fusion, f32[96]{0:T(128)S(1)} %get-tuple-element.2439), channel_id=1, replica_groups=mesh['types'=16,'tm'=2] {'types','tm'}, use_global_device_ids=true, to_apply=%region_31.32 | all-reduce | flops 104 | bytes 832 | tf_op jit(solution)/shard_map/psum | solution.py:200
  (2652 shorter events, 654.6 us)
Async XLA Ops:
  0.6 476.3 %copy-start = (f32[8,8]{1,0:T(8,128)S(1)}, f32[8,8]{1,0:T(8,128)}, u32[]{:S(2)}) copy-start(f32[8,8]{1,0:T(8,128)} %param.46) | copy-start | bytes 772
  0.6 10.4 %all-to-all-start = ((s32[6,4,7,512]{3,1,2,0:T(4,128)}), s32[6,4,7,512]{3,1,2,0:T(4,128)S(1)}, u32[]{:S(2)}, u32[]{:S(2)}) async-start(s32[6,4,7,512]{3,1,2,0:T(4,128)} %param.36), calls=%async_computation | async-start | bytes 688128 | tf_op jit(solution)/shard_map/all_to_all | solution.py:133
  4.1 0.7 copy-start.3
  4.8 0.7 copy-start.8
  7.4 0.7 copy-start.5
  8.9 0.7 copy-start.2
  9.6 0.7 copy-start.4
  10.3 0.7 copy-start.7
  11.3 0.7 copy-start.6
  12.0 147.6 %copy-start.1 = (f32[6,7,512]{2,1,0:T(8,128)S(1)}, f32[6,7,512]{2,1,0:T(8,128)}, u32[]{:S(2)}) copy-start(f32[6,7,512]{2,1,0:T(8,128)} %param.38) | copy-start | bytes 258052
  302.9 174.0 %copy-start.10 = (f32[8]{0:T(128)S(1)}, f32[8]{0:T(128)}, u32[]{:S(2)}) copy-start(f32[8]{0:T(128)} %param.44) | copy-start | bytes 100
  982.5 0.7 copy-start.9
  984.1 0.5 copy-start.11
where the time goes:
time: 992 us; the launch traced here: 985 us
  blocking collectives  387 us (39%)
  loops' own time  232 us (23%)
  matrix products  142 us (14%)
  other arithmetic  126 us (13%)
  local copies, waits for them, and re-layouts  92.5 us (9%)
    psum x2, blocking collectives, body(): totals = lax.psum(local_sum, ('types', 'tm'))  220 us
    all_gather x1, blocking collectives, body(): lax.all_gather(solve_type_series, ('types', 'tm'), axis=0, tiled=True)  166 us
    another operation x48, loops' own time, forward_period(): lax.fori_loop(0, blocks, forward_block_rows, jnp.zeros_like(weights))  98.9 us
    another operation x48, loops' own time, backward_period(): lax.fori_loop(0, blocks, backward_block_rows, (zeros_rows, zeros_rows, on...  95.8 us
    broadcast_in_dim x48, other arithmetic, forward_type(): lax.scan(forward_period, mass_start, (bracket, weight_up, savings, spendi...  64.1 us
    dot_general x96, matrix products, backward_block_rows(): jnp.einsum('eia,cea->cei', onehot, stacked_window, precision=highest)  53.3 us
    dot_general x96, matrix products, forward_block_rows(): contrib = jnp.einsum('eia,cei->cea', onehot, weight_rows, precision=highest)  39.9 us
    dot_general x48, matrix products, backward_period(): expected = patience * jnp.dot(transition, values, precision=highest)  37.1 us
  transfers between devices with their start and end apart: 1, of which 0 were waited for; matrix products, arithmetic and copies ran while one was open for 0% of the time, Pallas kernels for 0%

commit v1 on v0

--- a/solution.py
+++ b/solution.py
@@ -197,7 +197,7 @@
             ),
         )
         local_sum = jnp.sum(solve_type_series[:, 0, :], axis=0)
-        totals = lax.psum(local_sum, ("types", "tm"))
+        totals = lax.psum(lax.psum(local_sum, "tm"), axis_name="types")
         if newton_round + 1 == NEWTON:
             everything = (
                 lax.all_gather(solve_type_series, ("types", "tm"), axis=0, tiled=True),

time: 992 us -> 1020 us (1.028); the launches traced: 985 us -> 997 us
  blocking collectives: 387 us -> 408 us
    unnamed x0 -> x1, blocking collectives: none -> 46.2 us
    psum x2 -> x4, blocking collectives: 220 us -> 196 us  [body(): totals = lax.psum(lax.psum(local_sum, 'tm'), axis_name='types')]
where the time goes in v1:
time: 1020 us; the launch traced here: 997 us
  blocking collectives  408 us (40%)
  loops' own time  226 us (22%)
  matrix products  142 us (14%)
  other arithmetic  121 us (12%)
  local copies, waits for them, and re-layouts  93.3 us (9%)
    psum x4, blocking collectives, body(): totals = lax.psum(lax.psum(local_sum, 'tm'), axis_name='types')  196 us
    all_gather x1, blocking collectives, body(): lax.all_gather(solve_type_series, ('types', 'tm'), axis=0, tiled=True)  165 us
    another operation x48, loops' own time, forward_period(): lax.fori_loop(0, blocks, forward_block_rows, jnp.zeros_like(weights))  98.9 us
    another operation x48, loops' own time, backward_period(): lax.fori_loop(0, blocks, backward_block_rows, (zeros_rows, zeros_rows, on...  87 us
    broadcast_in_dim x48, other arithmetic, forward_type(): lax.scan(forward_period, mass_start, (bracket, weight_up, savings, spendi...  61.4 us
    dot_general x96, matrix products, backward_block_rows(): jnp.einsum('eia,cea->cei', onehot, stacked_window, precision=highest)  53.3 us
    unnamed x1, blocking collectives  46.2 us
    dot_general x96, matrix products, forward_block_rows(): contrib = jnp.einsum('eia,cei->cea', onehot, weight_rows, precision=highest)  39.9 us
  transfers between devices with their start and end apart: 1, of which 0 were waited for; matrix products, arithmetic and copies ran while one was open for 0% of the time, Pallas kernels for 0%

profile of v1, /device:TPU:14, one launch (start us, length us, event | category | flops | bytes accessed | tf_op | source)
XLA Modules:
  0.0 997.1 jit_solution(14698498611541894410)
XLA Ops:
  0.6 3.5 all-to-all-start
  12.0 145.1 %while.321 = (s32[]{:T(128)}, f32[3,8,7,512]{3,2,1,0:T(8,128)S(1)}, f32[3,8,7,512]{3,2,1,0:T(8,128)S(1)}, f32[3,8,7,512]{3,2,1,0:T(8,128)S(1)}, f32[3,7,512]{2,1...) while((s32[]{:T(128)}, f32[3,8,7,512]{3,2,1,0:T(8,128)S(1)}, ...), condition=%wide.region_5.6_spmd, body=%wide.region_0.5_spmd.sunk | while | flops 6097422 | bytes 1872705 | solution.py:173
  13.3 47.0 %while.328 = (s32[]{:T(128)}, f32[7,512]{1,0:T(8,128)S(1)}, f32[8,7,512]{2,1,0:T(8,128)S(1)}, f32[8,7,512]{2,1,0:T(8,128)S(1)}, f32[8,7,512]{2,1,0:T(8,128)S(1)}...) while((s32[]{:T(128)}, f32[7,512]{1,0:T(8,128)S(1)}, ...), condition=%wide.region_4.4_spmd.clone.clone, body=%wide.region_1.3_spmd.clone.clone.sunk | while | flops 6097420 | bytes 483244 | solution.py:77
  61.7 47.0 %while.328 = (s32[]{:T(128)}, f32[7,512]{1,0:T(8,128)S(1)}, f32[8,7,512]{2,1,0:T(8,128)S(1)}, f32[8,7,512]{2,1,0:T(8,128)S(1)}, f32[8,7,512]{2,1,0:T(8,128)S(1)}...) while((s32[]{:T(128)}, f32[7,512]{1,0:T(8,128)S(1)}, ...), condition=%wide.region_4.4_spmd.clone.clone, body=%wide.region_1.3_spmd.clone.clone.sunk | while | flops 6097420 | bytes 483244 | solution.py:77
  110.0 47.0 %while.328 = (s32[]{:T(128)}, f32[7,512]{1,0:T(8,128)S(1)}, f32[8,7,512]{2,1,0:T(8,128)S(1)}, f32[8,7,512]{2,1,0:T(8,128)S(1)}, f32[8,7,512]{2,1,0:T(8,128)S(1)}...) while((s32[]{:T(128)}, f32[7,512]{1,0:T(8,128)S(1)}, ...), condition=%wide.region_4.4_spmd.clone.clone, body=%wide.region_1.3_spmd.clone.clone.sunk | while | flops 6097420 | bytes 483244 | solution.py:77
  157.2 140.8 %while.323 = (s32[]{:T(128)}, f32[3,2,8]{2,1,0:T(2,128)S(1)}, f32[3,7,512]{2,1,0:T(8,128)S(1)}, s32[3,8,7,512]{3,2,1,0:T(8,128)S(1)}, f32[3,8,7,512]{3,2,1,0:T(8...) while((s32[]{:T(128)}, f32[3,2,8]{2,1,0:T(2,128)S(1)}, ...), condition=%wide.region_13.14_spmd, body=%wide.region_6.13_spmd.sunk | while | flops 6075148 | bytes 1450953 | solution.py:188
  157.9 46.2 %while.329 = (s32[]{:T(128)}, f32[7,512]{1,0:T(8,128)S(1)}, f32[8,2]{1,0:T(8,128)S(1)}, s32[8,7,512]{2,1,0:T(8,128)S(1)}, f32[8,7,512]{2,1,0:T(8,128)S(1)}, /*in...) while((s32[]{:T(128)}, f32[7,512]{1,0:T(8,128)S(1)}, ...), condition=%wide.region_12.12_spmd, body=%wide.region_7.11_spmd.sunk | while | flops 6075146 | bytes 502252 | solution.py:103
  158.6 3.4 while.334
  164.4 3.4 while.334
  170.2 3.4 while.334
  176.0 3.4 while.334
  181.7 3.4 while.334
  187.5 3.4 while.334
  193.3 3.4 while.334
  204.8 46.2 %while.329 = (s32[]{:T(128)}, f32[7,512]{1,0:T(8,128)S(1)}, f32[8,2]{1,0:T(8,128)S(1)}, s32[8,7,512]{2,1,0:T(8,128)S(1)}, f32[8,7,512]{2,1,0:T(8,128)S(1)}, /*in...) while((s32[]{:T(128)}, f32[7,512]{1,0:T(8,128)S(1)}, ...), condition=%wide.region_12.12_spmd, body=%wide.region_7.11_spmd.sunk | while | flops 6075146 | bytes 502252 | solution.py:103
  246.0 3.4 while.334
  251.8 46.2 %while.329 = (s32[]{:T(128)}, f32[7,512]{1,0:T(8,128)S(1)}, f32[8,2]{1,0:T(8,128)S(1)}, s32[8,7,512]{2,1,0:T(8,128)S(1)}, f32[8,7,512]{2,1,0:T(8,128)S(1)}, /*in...) while((s32[]{:T(128)}, f32[7,512]{1,0:T(8,128)S(1)}, ...), condition=%wide.region_12.12_spmd, body=%wide.region_7.11_spmd.sunk | while | flops 6075146 | bytes 502252 | solution.py:103
  300.5 162.3 %psum.29 = f32[8]{0:T(128)S(1)} all-reduce(f32[8]{0:T(128)S(1)} %psum.28), channel_id=1, replica_groups=mesh['types'=16,'tm'=2] {'types'}, use_global_device_ids=true, to_apply=%region_16.17 | all-reduce | flops 8 | bytes 64 | tf_op jit(solution)/shard_map/psum | solution.py:200
  465.1 145.1 %while.325 = (s32[]{:T(128)}, f32[3,8,7,512]{3,2,1,0:T(8,128)S(1)}, f32[3,8,7,512]{3,2,1,0:T(8,128)S(1)}, f32[3,8,7,512]{3,2,1,0:T(8,128)S(1)}, f32[3,7,512]{2,1...) while((s32[]{:T(128)}, f32[3,8,7,512]{3,2,1,0:T(8,128)S(1)}, ...), condition=%wide.region_22.23_spmd, body=%wide.region_17.22_spmd.sunk | while | flops 6097422 | bytes 1872697 | solution.py:173
  466.4 47.0 %while.330 = (s32[]{:T(128)}, f32[7,512]{1,0:T(8,128)S(1)}, f32[8,7,512]{2,1,0:T(8,128)S(1)}, f32[8,7,512]{2,1,0:T(8,128)S(1)}, f32[8,7,512]{2,1,0:T(8,128)S(1)}...) while((s32[]{:T(128)}, f32[7,512]{1,0:T(8,128)S(1)}, ...), condition=%wide.region_21.21_spmd.clone.clone, body=%wide.region_18.20_spmd.clone.clone.sunk | while | flops 6097420 | bytes 483244 | solution.py:77
  514.8 47.0 %while.330 = (s32[]{:T(128)}, f32[7,512]{1,0:T(8,128)S(1)}, f32[8,7,512]{2,1,0:T(8,128)S(1)}, f32[8,7,512]{2,1,0:T(8,128)S(1)}, f32[8,7,512]{2,1,0:T(8,128)S(1)}...) while((s32[]{:T(128)}, f32[7,512]{1,0:T(8,128)S(1)}, ...), condition=%wide.region_21.21_spmd.clone.clone, body=%wide.region_18.20_spmd.clone.clone.sunk | while | flops 6097420 | bytes 483244 | solution.py:77
  563.1 47.0 %while.330 = (s32[]{:T(128)}, f32[7,512]{1,0:T(8,128)S(1)}, f32[8,7,512]{2,1,0:T(8,128)S(1)}, f32[8,7,512]{2,1,0:T(8,128)S(1)}, f32[8,7,512]{2,1,0:T(8,128)S(1)}...) while((s32[]{:T(128)}, f32[7,512]{1,0:T(8,128)S(1)}, ...), condition=%wide.region_21.21_spmd.clone.clone, body=%wide.region_18.20_spmd.clone.clone.sunk | while | flops 6097420 | bytes 483244 | solution.py:77
  610.2 140.8 %while.327 = (s32[]{:T(128)}, f32[3,2,8]{2,1,0:T(2,128)S(1)}, f32[3,7,512]{2,1,0:T(8,128)S(1)}, s32[3,8,7,512]{3,2,1,0:T(8,128)S(1)}, f32[3,8,7,512]{3,2,1,0:T(8...) while((s32[]{:T(128)}, f32[3,2,8]{2,1,0:T(2,128)S(1)}, ...), condition=%wide.region_30.31_spmd, body=%wide.region_23.30_spmd.sunk | while | flops 6075148 | bytes 1450953 | solution.py:188
  610.9 46.2 %while.331 = (s32[]{:T(128)}, f32[7,512]{1,0:T(8,128)S(1)}, f32[8,2]{1,0:T(8,128)S(1)}, s32[8,7,512]{2,1,0:T(8,128)S(1)}, f32[8,7,512]{2,1,0:T(8,128)S(1)}, /*in...) while((s32[]{:T(128)}, f32[7,512]{1,0:T(8,128)S(1)}, ...), condition=%wide.region_29.29_spmd, body=%wide.region_24.28_spmd.sunk | while | flops 6075146 | bytes 502252 | solution.py:103
  611.7 3.4 while.332
  657.9 46.2 %while.331 = (s32[]{:T(128)}, f32[7,512]{1,0:T(8,128)S(1)}, f32[8,2]{1,0:T(8,128)S(1)}, s32[8,7,512]{2,1,0:T(8,128)S(1)}, f32[8,7,512]{2,1,0:T(8,128)S(1)}, /*in...) while((s32[]{:T(128)}, f32[7,512]{1,0:T(8,128)S(1)}, ...), condition=%wide.region_29.29_spmd, body=%wide.region_24.28_spmd.sunk | while | flops 6075146 | bytes 502252 | solution.py:103
  681.7 3.4 while.332
  699.0 3.4 while.332
  704.8 46.2 %while.331 = (s32[]{:T(128)}, f32[7,512]{1,0:T(8,128)S(1)}, f32[8,2]{1,0:T(8,128)S(1)}, s32[8,7,512]{2,1,0:T(8,128)S(1)}, f32[8,7,512]{2,1,0:T(8,128)S(1)}, /*in...) while((s32[]{:T(128)}, f32[7,512]{1,0:T(8,128)S(1)}, ...), condition=%wide.region_29.29_spmd, body=%wide.region_24.28_spmd.sunk | while | flops 6075146 | bytes 502252 | solution.py:103
  751.1 165.4 %all_gather.7 = f32[96,2,8]{2,1,0:T(2,128)S(1)} all-gather(f32[3,2,8]{2,1,0:T(2,128)S(1)} %get-tuple-element.1994), channel_id=1, replica_groups=mesh['types'=16,'tm'=2] {'types','tm'}, dimensions={0}, use_global_device_ids=true | all-gather | bytes 6336 | tf_op jit(solution)/shard_map/all_gather | solution.py:203
  916.7 46.2 %all-reduce.2 = f32[96]{0:T(128)S(1)} all-reduce(f32[96]{0:T(128)S(1)} %dynamic-slice_dynamic-update-slice_fusion), channel_id=1, replica_groups=mesh['types'=16,'tm'=2] {'types','tm'}, use_global_device_ids=true, to_apply=%add.2 | all-reduce | flops 96 | bytes 768
  966.9 29.1 %psum.31 = f32[8]{0:T(128)S(1)} all-reduce(f32[8]{0:T(128)S(1)} %psum.30), channel_id=1, replica_groups=mesh['types'=16,'tm'=2] {'types'}, use_global_device_ids=true, to_apply=%region_33.34 | all-reduce | flops 8 | bytes 64 | tf_op jit(solution)/shard_map/psum | solution.py:200
  (2656 shorter events, 652.5 us)
Async XLA Ops:
  0.6 462.1 %copy-start = (f32[8,8]{1,0:T(8,128)S(1)}, f32[8,8]{1,0:T(8,128)}, u32[]{:S(2)}) copy-start(f32[8,8]{1,0:T(8,128)} %param.46) | copy-start | bytes 772
  0.6 10.4 %all-to-all-start = ((s32[6,4,7,512]{3,1,2,0:T(4,128)}), s32[6,4,7,512]{3,1,2,0:T(4,128)S(1)}, u32[]{:S(2)}, u32[]{:S(2)}) async-start(s32[6,4,7,512]{3,1,2,0:T(4,128)} %param.36), calls=%async_computation | async-start | bytes 688128 | tf_op jit(solution)/shard_map/all_to_all | solution.py:133
  4.1 0.7 copy-start.5
  4.8 0.7 copy-start.8
  7.4 0.7 copy-start.4
  8.1 0.7 copy-start.3
  9.5 0.7 copy-start.2
  10.3 0.7 copy-start.7
  11.3 0.7 copy-start.6
  12.0 145.2 %copy-start.1 = (f32[6,7,512]{2,1,0:T(8,128)S(1)}, f32[6,7,512]{2,1,0:T(8,128)}, u32[]{:S(2)}) copy-start(f32[6,7,512]{2,1,0:T(8,128)} %param.38) | copy-start | bytes 258052
  300.5 162.3 %copy-start.10 = (f32[8]{0:T(128)S(1)}, f32[8]{0:T(128)}, u32[]{:S(2)}) copy-start(f32[8]{0:T(128)} %param.44) | copy-start | bytes 100
  965.3 0.7 copy-start.9
  996.0 0.5 copy-start.11
